TPU v7x, 32 devices: a whole 2x2x4 slice. The times are simulated.
32 devices in a mesh: frame: 16 (over z, y, x), row: 2 (over core).
Axes of the slice: x: 2, y: 2, z: 4, core: 2. Of those that a mesh axis runs over, the one named last changes fastest.
Arguments:
- footage: float32 [64, 1024, 1024], P('frame', 'row'), may hold values from -30 to 30
Outputs:
- coefficients: float32 [64, 1024, 1024], P('frame', 'row')
- energies: float32 [4, 10], replicated
All inputs are finite; a program needn't handle non-finite values.
Results may differ from a plain program's by a relative error of at most 0.00007.
Values sent between devices are 32-bit elements; how exact they have to be, the bound alone decides.
A program may use at most 128 MiB of HBM per device.

v0:
```python
import jax
import jax.numpy as jnp
import numpy as np
from jax import lax
from jax.sharding import PartitionSpec as P

SLEVELS = 3
TLEVELS = 3
LIFT_ALPHA = -1.586134342
LIFT_BETA = -0.05298011854
LIFT_GAMMA = 0.8829110762
LIFT_DELTA = 0.4435068522
LIFT_ZETA = 1.149604398


def shifted(block, axis, distance):
    devices = range(lax.axis_size(axis))
    route = [(i - distance, i) for i in devices if i - distance in devices]
    return lax.ppermute(block, axis, route)


def mirror_after(values, along):
    length = values.shape[along]
    return jnp.concatenate(
        [
            lax.slice_in_dim(values, 1, length, axis=along),
            lax.slice_in_dim(values, length - 1, length, axis=along),
        ],
        axis=along,
    )


def mirror_before(values, along):
    length = values.shape[along]
    return jnp.concatenate(
        [
            lax.slice_in_dim(values, 0, 1, axis=along),
            lax.slice_in_dim(values, 0, length - 1, axis=along),
        ],
        axis=along,
    )


def weave_axis(even_part, odd_part, along):
    stacked = jnp.stack([even_part, odd_part], axis=along + 1)
    new_shape = list(even_part.shape)
    new_shape[along] = new_shape[along] * 2
    return stacked.reshape(tuple(new_shape))


def lift_pair(even_part, odd_part, take_next, take_prev):
    odd_part = odd_part + LIFT_ALPHA * (even_part + take_next(even_part))
    even_part = even_part + LIFT_BETA * (take_prev(odd_part) + odd_part)
    odd_part = odd_part + LIFT_GAMMA * (even_part + take_next(even_part))
    even_part = even_part + LIFT_DELTA * (take_prev(odd_part) + odd_part)
    return (even_part * LIFT_ZETA, odd_part * (1.0 / LIFT_ZETA))


def table_next(values):
    return np.concatenate([values[:, 1:], values[:, -1:]], axis=1)


def table_prev(values):
    return np.concatenate([values[:, :1], values[:, :-1]], axis=1)


def column_matrix(width):
    identity = np.eye(width)
    even_part = identity[:, 0::2]
    odd_part = identity[:, 1::2]
    odd_part = odd_part + LIFT_ALPHA * (even_part + table_next(even_part))
    even_part = even_part + LIFT_BETA * (table_prev(odd_part) + odd_part)
    odd_part = odd_part + LIFT_GAMMA * (even_part + table_next(even_part))
    even_part = even_part + LIFT_DELTA * (table_prev(odd_part) + odd_part)
    lifted = np.concatenate([even_part * LIFT_ZETA, odd_part * (1.0 / LIFT_ZETA)], axis=1)
    return jnp.asarray(lifted.astype(np.float32))


def spatial_inplace(block, levels):
    frame_count, row_count, width = block.shape
    mixed = jnp.dot(block, column_matrix(width), precision=lax.Precision.HIGHEST)
    paired = mixed.reshape(frame_count, row_count // 2, 2, width)
    low_rows, high_rows = lift_pair(paired[:, :, 0, :], paired[:, :, 1, :], rows_next, rows_prev)
    half_width = width // 2
    coarse = low_rows[..., :half_width]
    if levels > 1:
        coarse = spatial_inplace(coarse, levels - 1)
    upper_rows = weave_axis(coarse, low_rows[..., half_width:], 2)
    bottom = weave_axis(high_rows[..., :half_width], high_rows[..., half_width:], 2)
    return jnp.stack([upper_rows, bottom], axis=2).reshape(frame_count, row_count, width)


def temporal(planes_in, levels):
    even_part = planes_in[0::2]
    odd_part = planes_in[1::2]
    odd_part = odd_part - 0.5 * (even_part + mirror_after(even_part, 0))
    even_part = even_part + 0.25 * (mirror_before(odd_part, 0) + odd_part)
    if levels > 1:
        even_part = temporal(even_part, levels - 1)
    return weave_axis(even_part, odd_part, 0)


def rows_next(values):
    arrived = shifted(values[:, :1], "row", -1)
    is_last = lax.axis_index("row") == lax.axis_size("row") - 1
    return jnp.concatenate([values[:, 1:], jnp.where(is_last, values[:, -1:], arrived)], axis=1)


def rows_prev(values):
    arrived = shifted(values[:, -1:], "row", 1)
    is_first = lax.axis_index("row") == 0
    return jnp.concatenate([jnp.where(is_first, values[:, :1], arrived), values[:, :-1]], axis=1)


def level_of(number, ceiling):
    depth_now = 1
    while number % 2 == 0 and depth_now <= ceiling:
        number = number // 2
        depth_now = depth_now + 1
    return depth_now


def space_table(levels):
    period = 2**levels
    band_table = np.zeros((period * period, 3 * levels + 1), np.float32)
    for row_pos in range(period):
        for col_pos in range(period):
            row_level = level_of(row_pos, levels)
            col_level = level_of(col_pos, levels)
            finest = min(row_level, col_level)
            if finest > levels:
                column = 3 * levels
            elif row_level == col_level:
                column = 3 * (finest - 1) + 2
            elif row_level == finest:
                column = 3 * (finest - 1)
            else:
                column = 3 * (finest - 1) + 1
            band_table[row_pos * period + col_pos, column] = 1.0
    return band_table


def time_table(levels):
    period = 2**levels
    band_table = np.zeros((period, levels + 1), np.float32)
    for number in range(period):
        band_table[number, level_of(number, levels) - 1] = 1.0
    return band_table


def band_sums(coeffs, first_frame, levels_s, levels_t):
    period = 2**levels_s
    frame_count, row_count, col_count = coeffs.shape
    square = coeffs * coeffs
    row_folded = square.reshape(frame_count, row_count // period, period, col_count).sum(axis=1)
    column_phase = np.arange(col_count) % period
    selector = jnp.asarray((column_phase[:, None] == np.arange(period)[None, :]).astype(np.float32))
    pattern = jnp.dot(row_folded, selector, precision=lax.Precision.HIGHEST)
    pattern = pattern.reshape(frame_count, period * period)
    per_frame = jnp.dot(
        pattern, jnp.asarray(space_table(levels_s), jnp.float32), precision=lax.Precision.HIGHEST
    )
    time_period = 2**levels_t
    position = (first_frame + jnp.arange(frame_count, dtype=jnp.int32)) % time_period
    onehot = (position[:, None] == jnp.arange(time_period, dtype=jnp.int32)[None, :]).astype(
        jnp.float32
    )
    frame_band = jnp.dot(
        onehot, jnp.asarray(time_table(levels_t), jnp.float32), precision=lax.Precision.HIGHEST
    )
    return jnp.dot(frame_band.T, per_frame, precision=lax.Precision.HIGHEST)


def band_means(totals, frames_all, rows_all, cols_all, levels_s, levels_t):
    space_share = space_table(levels_s).sum(0) / float((2**levels_s) ** 2)
    time_share = time_table(levels_t).sum(0) / float(2**levels_t)
    counts = (
        float(frames_all) * float(rows_all) * float(cols_all) * np.outer(time_share, space_share)
    )
    return totals / jnp.asarray(counts, jnp.float32)


def shards(footage):
    frames_dev = footage.shape[0]
    planes = spatial_inplace(footage, SLEVELS)
    temporal_out = temporal(
        lax.all_to_all(planes, "frame", split_axis=1, concat_axis=0, tiled=True), TLEVELS
    )
    coeffs = lax.all_to_all(temporal_out, "frame", split_axis=0, concat_axis=1, tiled=True)
    totals = band_sums(coeffs, lax.axis_index("frame") * frames_dev, SLEVELS, TLEVELS)
    totals = lax.psum(totals, ("frame", "row"))
    means = band_means(
        totals,
        frames_dev * lax.axis_size("frame"),
        coeffs.shape[1] * lax.axis_size("row"),
        coeffs.shape[2],
        SLEVELS,
        TLEVELS,
    )
    return (coeffs, means)


def solution(mesh):
    return jax.shard_map(
        shards,
        mesh=mesh,
        in_specs=(P("frame", "row", None),),
        out_specs=(P("frame", "row", None), P()),
        check_vma=False,
    )
```

profile of v0, /device:TPU:14, one launch (start us, length us, event | category | flops | bytes accessed | tf_op | source)
XLA Modules:
  0.0 669.8 jit_solution(6688530232217569210)
XLA Ops:
  0.6 31.4 %convolution_bitcast_fusion = f32[4,512,1024]{2,1,0:T(8,128)} fusion(f32[1024,1024,1]{1,0,2:T(8,128)} %constant.85, f32[4,512,1024]{2,1,0:T(8,128)} %param.8), kind=kOutput, calls=%fused_computation.26 | convolution fusion | flops 25769803776 | bytes 20971520 | tf_op jit(solution)/shard_map/dot_general | solution.py:81
  32.0 10.6 %reshape.40 = f32[4,256,2,1024]{3,2,1,0:T(2,128)} reshape(f32[4,512,1024]{2,1,0:T(8,128)} %convolution_bitcast_fusion) | data formatting | bytes 16777216 | tf_op jit(solution)/shard_map/reshape | solution.py:82
  42.6 10.7 %fusion.50 = (f32[4,256,1,1024]{3,2,1,0:T(1,128)}, f32[4,256,1,1024]{3,2,1,0:T(1,128)S(1)}) fusion(f32[4,256,2,1024]{3,2,1,0:T(2,128)} %reshape.40), kind=kLoop, calls=%fused_computation.109 | loop fusion | bytes 16777216 | tf_op jit(solution)/shard_map/slice | solution.py:83
  57.4 2.5 slice.290
  60.8 7.3 %fusion.1 = f32[4,256,1024]{2,1,0:T(8,128)S(1)} fusion(f32[4,1,1024]{2,1,0:T(1,128)S(1)} %broadcast_select_fusion.1, f32[4,255,1024]{2,1,0:T(8,128)} %slice.290, f32[4,256,1,1024]{3,2,1,0:T(1,128)} %get-tuple-element.8, f32[4,256,1,1024]{3,2,1,0:T(1,128)} %copy-done.2), kind=kLoop, calls=%fused_computation.4 | loop fusion | flops 4194304 | bytes 16777216 | tf_op jit(solution)/shard_map/add | solution.py:52
  68.2 2.0 copy-done
  70.2 2.7 collective-permute-start.1
  74.3 6.8 %fusion.3 = f32[4,256,1024]{2,1,0:T(8,128)S(1)} fusion(f32[4,256,1024]{2,1,0:T(8,128)} %copy-done, f32[4,255,1024]{2,1,0:T(8,128)} %bitcast.99, f32[4,1,1024]{2,1,0:T(1,128)S(1)} %broadcast_select_fusion.3, f32[4,256,1,1024]{3,2,1,0:T(1,128)} %copy-done.2), kind=kLoop, calls=%fused_computation.7 | loop fusion | flops 4194304 | bytes 16777216 | tf_op jit(solution)/shard_map/add | solution.py:53
  81.1 1.6 collective-permute-start.2
  82.7 2.5 slice.296
  85.2 5.8 broadcast_multiply_fusion
  91.0 3.0 collective-permute-start.3
  94.9 1.6 fusion.8
  96.5 2.0 copy-done.5
  98.5 4.8 fusion.13
  103.4 2.5 reshape.41
  105.8 1.6 fusion.51
  107.6 1.6 collective-permute-start.4
  109.3 1.6 collective-permute-done.4
  111.3 2.1 collective-permute-start.5
  115.9 2.5 pad_maximum_fusion.3
  118.4 5.4 copy.49
  124.4 3.3 collective-permute-start.7
  127.8 1.5 slice_bitcast_fusion.2
  138.1 2.9 collective-permute-start.9
  144.7 1.7 collective-permute-done.10
  147.0 2.1 collective-permute-start.11
  155.5 1.4 pad_maximum_fusion.5
  156.8 2.4 copy.47
  159.2 3.9 stack_reshape.35
  163.1 4.2 pad_maximum_fusion.2
  167.3 5.5 copy.48
  172.9 8.8 %pad_maximum_fusion = f32[4,256,2,1024]{1,0,3,2:T(4,128)} fusion(f32[4,256,1,1024]{1,0,3,2:T(4,128)} %bitcast.112, f32[4,256,1,1024]{1,0,3,2:T(4,128)} %bitcast.113), kind=kLoop, calls=%fused_computation | loop fusion | flops 2097152 | bytes 16777216 | tf_op jit(solution)/shard_map/stack | solution.py:90
  181.7 11.4 %copy.50 = f32[4,256,2,1024]{3,0,2,1:T(4,128)} copy(f32[4,256,2,1024]{1,0,3,2:T(4,128)} %pad_maximum_fusion) | data formatting | bytes 16777216 | tf_op jit(solution)/shard_map/stack | solution.py:90
  193.1 189.2 %all_to_all.36 = f32[4,512,1024]{2,0,1:T(4,128)S(1)} all-to-all(f32[4,512,1024]{2,0,1:T(4,128)} %bitcast.104), channel_id=1, replica_groups=mesh['frame'=16,'row'=2] {'frame'}, dimensions={1} | all-to-all | bytes 16777216 | tf_op jit(solution)/shard_map/all_to_all | solution.py:187
  382.3 4.9 copy.51
  387.2 1.7 copy.52
  389.9 2.0 fusion.10
  392.4 2.0 fusion.12
  399.8 1.7 pad_maximum_fusion.1
  401.4 4.2 copy.55
  405.7 6.7 all-to-all-start.1
  412.6 184.9 %all-to-all-done.1 = f32[64,32,1024]{2,1,0:T(8,128)} async-done(((f32[64,32,1024]{2,1,0:T(8,128)}), f32[64,32,1024]{2,1,0:T(8,128)}, u32[]{:S(2)}, u32[]{:S(2)}) %all-to-all-start.1) | async-done | bytes 8388640 | tf_op jit(solution)/shard_map/all_to_all | solution.py:189
  597.5 12.0 %mul.203 = f32[4,16,32,1024]{3,2,0,1:T(8,128)} multiply(f32[4,16,32,1024]{3,2,0,1:T(8,128)} %bitcast.39, f32[4,16,32,1024]{3,2,0,1:T(8,128)} %bitcast.39) | non-fusion elementwise | flops 2097152 | bytes 25165824 | tf_op jit(solution)/shard_map/mul | solution.py:154
  609.5 8.6 %copy.56 = f32[4,16,32,1024]{3,2,1,0:T(8,128)} copy(f32[4,16,32,1024]{3,2,0,1:T(8,128)} %bitcast.39) | data formatting | bytes 16777216 | tf_op jit(solution)/shard_map/all_to_all | solution.py:189
  618.1 4.1 copy.57
  622.2 3.9 reduce_sum.9
  626.8 41.9 %psum.7 = f32[4,10]{1,0:T(4,128)S(1)} all-reduce(f32[4,10]{1,0:T(4,128)S(1)} %fusion.56), channel_id=1, replica_groups=mesh['frame'=16,'row'=2] {'frame','row'}, use_global_device_ids=true, to_apply=%region_1.2 | all-reduce | flops 40 | bytes 320 | tf_op jit(solution)/shard_map/psum | solution.py:191
  (138 shorter events, 38.4 us)
Async XLA Ops:
  53.3 2.0 copy-start.2
  55.4 2.0 copy-start.4
  55.4 4.5 collective-permute-start
  68.2 2.0 copy-start
  70.2 3.2 collective-permute-start.1
  81.1 4.1 copy-start.1
  81.1 4.1 collective-permute-start.2
  91.0 3.9 collective-permute-start.3
  94.9 3.6 copy-start.14
  96.5 2.0 copy-start.5
  107.5 5.9 copy-start.7
  107.6 3.3 collective-permute-start.4
  111.3 2.9 collective-permute-start.5
  114.6 9.3 %collective-permute-start.6 = (f32[4,1,512]{2,1,0:T(1,128)S(1)}, f32[4,1,512]{2,1,0:T(1,128)S(1)}, u32[]{:S(2)}, u32[]{:S(2)}) collective-permute-start(f32[4,1,512]{2,1,0:T(1,128)S(1)} %slice.313), channel_id=1, source_target_pairs={{1,0},{3,2},{5,4},{7,6},{9,8},{11,10},{13,12},{15,14},{17,16},{19,... | collective-permute-start | bytes 24584 | tf_op jit(solution)/shard_map/ppermute | solution.py:19
  123.8 3.9 copy-start.6
  124.4 5.3 copy-start.15
  124.4 4.8 collective-permute-start.7
  129.7 7.2 %copy-start.9 = (f32[4,128,512]{2,1,0:T(8,128)}, f32[4,128,512]{2,1,0:T(8,128)S(1)}, u32[]{:S(2)}) copy-start(f32[4,128,512]{2,1,0:T(8,128)S(1)} %fusion.27) | copy-start | bytes 3145732
  132.8 3.8 collective-permute-start.8
  135.7 5.3 copy-start.12
  135.7 5.3 copy-start.13
  138.1 4.0 collective-permute-start.9
  141.6 2.0 copy-start.10
  142.3 4.1 collective-permute-start.10
  147.0 3.6 collective-permute-start.11
  150.9 2.1 copy-start.11
  159.2 3.9 copy-start.8
  405.7 6.7 copy-start.19
  405.7 191.8 %all-to-all-start.1 = ((f32[64,32,1024]{2,1,0:T(8,128)}), f32[64,32,1024]{2,1,0:T(8,128)}, u32[]{:S(2)}, u32[]{:S(2)}) async-start(f32[64,32,1024]{2,1,0:T(8,128)} %bitcast.102), calls=%async_computation.1 | async-start | bytes 16777216 | tf_op jit(solution)/shard_map/all_to_all | solution.py:189
  609.5 8.6 %copy-start.3 = (f32[4,16,32,1024]{3,2,0,1:T(8,128)S(1)}, f32[4,16,32,1024]{3,2,0,1:T(8,128)}, u32[]{:S(2)}) copy-start(f32[4,16,32,1024]{3,2,0,1:T(8,128)} %mul.203) | copy-start | bytes 25165828
  622.2 3.9 copy-start.17
  622.2 4.3 copy-start.16
  622.2 46.5 %copy-start.18 = (f32[4,10]{1,0:T(4,128)S(1)}, f32[4,10]{1,0:T(4,128)}, u32[]{:S(2)}) copy-start(f32[4,10]{1,0:T(4,128)} %constant.84) | copy-start | bytes 484
where the time goes:
time: 680 us; the launch traced here: 670 us
  blocking collectives  231 us (34%)
  waiting for transfers between devices  192 us (28%)
  local copies, waits for them, and re-layouts  105 us (15%)
  other arithmetic  70.7 us (10%)
  matrix products  37.5 us (6%)
  starting transfers between devices  31 us (5%)
    all_to_all x1, blocking collectives, shards(): lax.all_to_all(planes, 'frame', split_axis=1, concat_axis=0, tiled=True)  189 us
    all_to_all x1, waiting for transfers between devices, shards(): lax.all_to_all(temporal_out, 'frame', split_axis=0, concat_axis=1, tiled=...  185 us
    psum x1, blocking collectives, shards(): totals = lax.psum(totals, ('frame', 'row'))  41.9 us
    dot_general x3, matrix products, spatial_inplace(): jnp.dot(block, column_matrix(width), precision=lax.Precision.HIGHEST)  36.7 us
    another operation x15, local copies, waits for them, and re-layouts, weave_axis(): stacked = jnp.stack([even_part, odd_part], axis=along + 1)  27.3 us
    ppermute x12, starting transfers between devices, shifted(): return lax.ppermute(block, axis, route)  24.3 us
    another operation x3, local copies, waits for them, and re-layouts, spatial_inplace(): jnp.stack([upper_rows, bottom], axis=2)  14.1 us
  transfers between devices with their start and end apart: 13, of which 9 were waited for; matrix products, arithmetic and copies ran while one was open for 3% of the time, Pallas kernels for 0%

commit v1 on v0

--- a/solution.py
+++ b/solution.py
@@ -186,7 +186,10 @@
     temporal_out = temporal(
         lax.all_to_all(planes, "frame", split_axis=1, concat_axis=0, tiled=True), TLEVELS
     )
-    coeffs = lax.all_to_all(temporal_out, "frame", split_axis=0, concat_axis=1, tiled=True)
+    count = lax.axis_size("frame")
+    shards_2 = jnp.stack(jnp.split(temporal_out, count, axis=0), axis=0)
+    shards_2 = lax.all_to_all(shards_2, "frame", split_axis=0, concat_axis=0)
+    coeffs = jnp.concatenate(shards_2, axis=1)
     totals = band_sums(coeffs, lax.axis_index("frame") * frames_dev, SLEVELS, TLEVELS)
     totals = lax.psum(totals, ("frame", "row"))
     means = band_means(

time: 680 us -> 681 us (level)
  local copies, waits for them, and re-layouts: 105 us -> 115 us
  other arithmetic: 70.7 us -> 62.2 us
    unnamed x44 -> x57, local copies, waits for them, and re-layouts: 8.26 us -> 20.8 us
    all_to_all x1 -> x0, local copies, waits for them, and re-layouts: 8.59 us -> none  [shards(): lax.all_to_all(temporal_out, 'frame', split_axis=0, concat_axis=1, tiled=...]
    reshape x0 -> x1, local copies, waits for them, and re-layouts: none -> 8.45 us  [shards(): coeffs = jnp.concatenate(shards_2, axis=1)]
    mul x1, other arithmetic: 12 us -> 4.35 us  [band_sums(): square = coeffs * coeffs]
    another operation x15 -> x14, local copies, waits for them, and re-layouts: 27.3 us -> 23.1 us  [weave_axis(): stacked = jnp.stack([even_part, odd_part], axis=along + 1)]
where the time goes in v1:
time: 681 us; the launch traced here: 671 us
  blocking collectives  231 us (34%)
  waiting for transfers between devices  192 us (28%)
  local copies, waits for them, and re-layouts  115 us (17%)
  other arithmetic  62.2 us (9%)
  matrix products  37.5 us (6%)
  starting transfers between devices  31 us (5%)
    all_to_all x1, blocking collectives, shards(): lax.all_to_all(planes, 'frame', split_axis=1, concat_axis=0, tiled=True)  189 us
    all_to_all x1, waiting for transfers between devices, shards(): shards_2 = lax.all_to_all(shards_2, 'frame', split_axis=0, concat_axis=0)  185 us
    psum x1, blocking collectives, shards(): totals = lax.psum(totals, ('frame', 'row'))  41.9 us
    dot_general x3, matrix products, spatial_inplace(): jnp.dot(block, column_matrix(width), precision=lax.Precision.HIGHEST)  36.7 us
    ppermute x12, starting transfers between devices, shifted(): return lax.ppermute(block, axis, route)  24.3 us
    another operation x14, local copies, waits for them, and re-layouts, weave_axis(): stacked = jnp.stack([even_part, odd_part], axis=along + 1)  23.1 us
    unnamed x57, local copies, waits for them, and re-layouts  20.8 us
    another operation x3, local copies, waits for them, and re-layouts, spatial_inplace(): jnp.stack([upper_rows, bottom], axis=2)  14.1 us
  transfers between devices with their start and end apart: 13, of which 9 were waited for; matrix products, arithmetic and copies ran while one was open for 3% of the time, Pallas kernels for 0%

profile of v1, /device:TPU:14, one launch (start us, length us, event | category | flops | bytes accessed | tf_op | source)
XLA Modules:
  0.0 671.3 jit_solution(5780232659680300098)
XLA Ops:
  0.6 31.4 %convolution_bitcast_fusion = f32[4,512,1024]{2,1,0:T(8,128)} fusion(f32[1024,1024,1]{1,0,2:T(8,128)} %constant.85, f32[4,512,1024]{2,1,0:T(8,128)} %param.8), kind=kOutput, calls=%fused_computation.55 | convolution fusion | flops 25769803776 | bytes 20971520 | tf_op jit(solution)/shard_map/dot_general | solution.py:81
  32.0 10.7 %reshape.76 = f32[4,256,2,1024]{3,2,1,0:T(2,128)} reshape(f32[4,512,1024]{2,1,0:T(8,128)} %convolution_bitcast_fusion) | data formatting | bytes 16777216 | tf_op jit(solution)/shard_map/reshape | solution.py:82
  42.6 10.7 %fusion.65 = (f32[4,256,1,1024]{3,2,1,0:T(1,128)}, f32[4,256,1,1024]{3,2,1,0:T(1,128)S(1)}) fusion(f32[4,256,2,1024]{3,2,1,0:T(2,128)} %reshape.76), kind=kLoop, calls=%fused_computation.171 | loop fusion | bytes 16777216 | tf_op jit(solution)/shard_map/slice | solution.py:83
  55.4 1.3 collective-permute-start
  57.4 2.5 slice.306
  60.9 7.3 %fusion.1 = f32[4,256,1024]{2,1,0:T(8,128)S(1)} fusion(f32[4,1,1024]{2,1,0:T(1,128)S(1)} %broadcast_select_fusion.1, f32[4,255,1024]{2,1,0:T(8,128)} %slice.306, f32[4,256,1,1024]{3,2,1,0:T(1,128)} %get-tuple-element.24, f32[4,256,1,1024]{3,2,1,0:T(1,128)} %copy-done.2), kind=kLoop, calls=%fused_computation.33 | loop fusion | flops 4194304 | bytes 16777216 | tf_op jit(solution)/shard_map/add | solution.py:52
  68.2 2.0 copy-done
  70.2 2.7 collective-permute-start.1
  74.3 6.8 %fusion.3 = f32[4,256,1024]{2,1,0:T(8,128)S(1)} fusion(f32[4,256,1024]{2,1,0:T(8,128)} %copy-done, f32[4,255,1024]{2,1,0:T(8,128)} %bitcast.147, f32[4,1,1024]{2,1,0:T(1,128)S(1)} %broadcast_select_fusion.3, f32[4,256,1,1024]{3,2,1,0:T(1,128)} %copy-done.2), kind=kLoop, calls=%fused_computation.36 | loop fusion | flops 4194304 | bytes 16777216 | tf_op jit(solution)/shard_map/add | solution.py:53
  81.2 1.6 collective-permute-start.2
  82.8 2.5 slice.312
  85.3 5.8 broadcast_multiply_fusion
  91.1 3.0 collective-permute-start.3
  95.0 1.6 fusion.8
  96.6 2.0 copy-done.4
  98.6 4.8 fusion.13
  103.4 2.5 reshape.77
  105.9 1.6 fusion.66
  107.7 1.6 collective-permute-start.4
  109.4 1.6 collective-permute-done.4
  111.4 2.1 collective-permute-start.5
  116.0 2.5 pad_maximum_fusion.2
  118.5 5.5 copy.82
  124.5 3.3 collective-permute-start.7
  127.9 1.5 slice_bitcast_fusion.2
  138.2 2.9 collective-permute-start.9
  144.7 1.7 collective-permute-done.10
  147.1 2.1 collective-permute-start.11
  154.2 1.3 copy.78
  155.5 1.4 pad_maximum_fusion.4
  156.9 2.4 copy.80
  159.3 3.9 stack_reshape.35
  163.2 4.2 pad_maximum_fusion.1
  167.5 5.5 copy.81
  173.0 8.8 %pad_maximum_fusion = f32[4,256,2,1024]{1,0,3,2:T(4,128)} fusion(f32[4,256,1,1024]{1,0,3,2:T(4,128)} %bitcast.160, f32[4,256,1,1024]{1,0,3,2:T(4,128)} %bitcast.161), kind=kLoop, calls=%fused_computation.30 | loop fusion | flops 2097152 | bytes 16777216 | tf_op jit(solution)/shard_map/stack | solution.py:90
  181.8 11.4 %copy.83 = f32[4,256,2,1024]{3,0,2,1:T(4,128)} copy(f32[4,256,2,1024]{1,0,3,2:T(4,128)} %pad_maximum_fusion) | data formatting | bytes 16777216 | tf_op jit(solution)/shard_map/stack | solution.py:90
  193.2 189.2 %all_to_all.23 = f32[4,512,1024]{2,0,1:T(4,128)S(1)} all-to-all(f32[4,512,1024]{2,0,1:T(4,128)} %bitcast.152), channel_id=1, replica_groups=mesh['frame'=16,'row'=2] {'frame'}, dimensions={1} | all-to-all | bytes 16777216 | tf_op jit(solution)/shard_map/all_to_all | solution.py:187
  382.4 4.9 copy.84
  387.3 1.7 copy.85
  390.0 2.0 fusion.10
  392.5 2.0 fusion.12
  414.9 6.7 all-to-all-start.1
  421.7 185.0 %all-to-all-done.1 = f32[16,4,32,1024]{3,2,1,0:T(8,128)} async-done(((f32[16,4,32,1024]{3,2,1,0:T(8,128)}), f32[16,4,32,1024]{3,2,1,0:T(8,128)}, u32[]{:S(2)}, u32[]{:S(2)}) %all-to-all-start.1) | async-done | bytes 8388640 | tf_op jit(solution)/shard_map/all_to_all | solution.py:191
  606.7 4.4 bitcast_multiply_fusion
  611.1 4.2 copy.105
  615.3 3.9 reduce_sum.9
  619.9 41.9 %psum.7 = f32[4,10]{1,0:T(4,128)S(1)} all-reduce(f32[4,10]{1,0:T(4,128)S(1)} %fusion.71), channel_id=1, replica_groups=mesh['frame'=16,'row'=2] {'frame','row'}, use_global_device_ids=true, to_apply=%region_1.2 | all-reduce | flops 40 | bytes 320 | tf_op jit(solution)/shard_map/psum | solution.py:194
  661.8 8.5 %copy.104 = f32[4,16,32,1024]{3,2,1,0:T(8,128)} copy(f32[4,16,32,1024]{3,2,0,1:T(8,128)} %bitcast.53) | data formatting | bytes 16777216 | tf_op jit(solution)/shard_map/reshape | solution.py:192
  (168 shorter events, 50.7 us)
Async XLA Ops:
  53.3 2.1 copy-start.2
  55.4 2.0 copy-start.3
  55.4 4.5 collective-permute-start
  68.2 2.0 copy-start
  70.2 3.2 collective-permute-start.1
  81.2 4.1 copy-start.1
  81.2 4.1 collective-permute-start.2
  91.1 3.9 collective-permute-start.3
  95.0 3.6 copy-start.13
  96.6 2.0 copy-start.4
  107.5 5.9 copy-start.6
  107.7 3.3 collective-permute-start.4
  111.4 2.9 collective-permute-start.5
  114.7 9.3 %collective-permute-start.6 = (f32[4,1,512]{2,1,0:T(1,128)S(1)}, f32[4,1,512]{2,1,0:T(1,128)S(1)}, u32[]{:S(2)}, u32[]{:S(2)}) collective-permute-start(f32[4,1,512]{2,1,0:T(1,128)S(1)} %slice.329), channel_id=1, source_target_pairs={{1,0},{3,2},{5,4},{7,6},{9,8},{11,10},{13,12},{15,14},{17,16},{19,... | collective-permute-start | bytes 24584 | tf_op jit(solution)/shard_map/ppermute | solution.py:19
  123.9 3.9 copy-start.5
  124.5 5.3 copy-start.14
  124.5 4.8 collective-permute-start.7
  129.8 7.2 %copy-start.8 = (f32[4,128,512]{2,1,0:T(8,128)}, f32[4,128,512]{2,1,0:T(8,128)S(1)}, u32[]{:S(2)}) copy-start(f32[4,128,512]{2,1,0:T(8,128)S(1)} %fusion.27) | copy-start | bytes 3145732
  132.9 3.8 collective-permute-start.8
  135.7 5.3 copy-start.11
  135.8 5.3 copy-start.12
  138.2 4.0 collective-permute-start.9
  141.7 2.0 copy-start.9
  142.4 4.1 collective-permute-start.10
  147.1 3.6 collective-permute-start.11
  151.0 2.1 copy-start.10
  159.3 3.9 copy-start.7
  414.9 6.7 copy-start.18
  414.9 191.8 %all-to-all-start.1 = ((f32[16,4,32,1024]{3,2,1,0:T(8,128)}), f32[16,4,32,1024]{3,2,1,0:T(8,128)}, u32[]{:S(2)}, u32[]{:S(2)}) async-start(f32[16,4,32,1024]{3,2,1,0:T(8,128)} %bitcast_dynamic-update-slice_fusion), calls=%async_computation.1 | async-start | bytes 16777216 | tf_op jit(solution)/shard_map/all_to_all | solution.py:191
  615.3 3.9 copy-start.16
  615.3 4.2 copy-start.15
  661.8 8.5 %copy-start.17 = (f32[4,10]{1,0:T(4,128)S(1)}, f32[4,10]{1,0:T(4,128)}, u32[]{:S(2)}) copy-start(f32[4,10]{1,0:T(4,128)} %constant.84) | copy-start | bytes 484
